TPU v7x, 32 devices: a whole 2x2x4 slice. The times are simulated.
32 devices in a mesh: gx: 4 (over z), gy: 4 (over y, x), gz: 2 (over core).
Axes of the slice: x: 2, y: 2, z: 4, core: 2. Of those that a mesh axis runs over, the one named last changes fastest.
Arguments:
- panel: float32 [8192, 4096], P(('gx', 'gy', 'gz'))
- treat_start: int32 [8192], P(('gx', 'gy', 'gz')), may hold values from 1024 to 4096
- loading_init: float32 [64, 8192], P(None, ('gx', 'gy', 'gz'))
- factor_init: float32 [64, 4096], P(None, ('gx', 'gy', 'gz'))
- unit_init: float32 [8192], P(('gx', 'gy', 'gz'))
- day_init: float32 [4096], replicated
Outputs:
- loading_out: float32 [64, 8192], P(None, ('gx', 'gy', 'gz'))
- factor_out: float32 [64, 4096], P(None, ('gx', 'gy', 'gz'))
- unit_out: float32 [8192], P(('gx', 'gy', 'gz'))
- day_out: float32 [4096], replicated
Inputs may be any that keep to these rules, and one draw needn't show every extreme that they name: A unit is treated from day treat_start on; 4096 means never treated.
All inputs are finite; a program needn't handle non-finite values.
Results may differ from a plain program's by a relative error of at most 0.0001.
Values sent between devices are 32-bit elements; how exact they have to be, the bound alone decides.
A program may use at most 64 MiB of HBM per device.

v0:
```python
import functools

import jax
import jax.numpy as jnp
from jax import lax
from jax.experimental import pallas as pl
from jax.experimental.pallas import tpu as pltpu
from jax.sharding import PartitionSpec as P

SWEEPS = 2
RIDGE = 1.0
AXES = ("gx", "gy", "gz")
MESH = pl.DeviceIdType.MESH
VMEM = pl.BlockSpec(memory_space=pltpu.VMEM)


def peers(shape):
    here = {axis: lax.axis_index(axis) for axis in AXES}
    found = {}
    for axis in AXES:
        found[axis] = []
        for step in range(1, shape[axis]):
            there = dict(here)
            there[axis] = lax.rem(here[axis] + step, shape[axis])
            found[axis].append((step, there[axis], tuple(there[name] for name in AXES)))
    return here, found


def meet(found):
    barrier = pltpu.get_barrier_semaphore()
    count = 0
    for axis in AXES:
        for _, _, device in found[axis]:
            pl.semaphore_signal(barrier, inc=1, device_id=device, device_id_type=MESH)
            count += 1
    pl.semaphore_wait(barrier, count)


def spread(out_ref, here, found, send, recv, base):
    index = base
    for depth, axis in ((3, "gx"), (2, "gy"), (1, "gz")):
        at = (here["gz"], here["gy"], here["gx"])[:depth]
        mine = out_ref.at[at]
        copies = []
        for _, _, device in found[axis]:
            copies.append(pltpu.make_async_remote_copy(
                mine, mine, send.at[index], recv.at[index], device_id=device, device_id_type=MESH))
            index += 1
        for copy in copies:
            copy.start()
        for copy in copies:
            copy.wait()


def gather_kernel(shape, own_ref, out_ref, send, recv, local):
    here, found = peers(shape)
    copy = pltpu.make_async_copy(own_ref, out_ref.at[here["gz"], here["gy"], here["gx"]], local)
    copy.start()
    meet(found)
    copy.wait()
    spread(out_ref, here, found, send, recv, 0)


def reduce_kernel(shape, part_ref, out_ref, hold_z, hold_y, hold_x, sum_z, sum_y, send, recv):
    here, found = peers(shape)
    meet(found)
    source = part_ref
    index = 0
    for axis, hold, total in (("gz", hold_z, sum_z), ("gy", hold_y, sum_y), ("gx", hold_x, None)):
        copies = []
        for step, there, device in found[axis]:
            copies.append(pltpu.make_async_remote_copy(
                source.at[there], hold.at[step - 1], send.at[index], recv.at[index],
                device_id=device, device_id_type=MESH))
            index += 1
        for copy in copies:
            copy.start()
        for copy in copies:
            copy.wait()
        value = source[here[axis]]
        for slot in range(len(copies)):
            value = value + hold[slot]
        if total is None:
            out_ref[here["gz"], here["gy"], here["gx"]] = value
        else:
            total[...] = value
            source = total
    spread(out_ref, here, found, send, recv, index)


def links(shape):
    return sum(shape[axis] - 1 for axis in AXES)


def gather(shape, own):
    sizes = (shape["gz"], shape["gy"], shape["gx"])
    count = links(shape)
    return pl.pallas_call(
        functools.partial(gather_kernel, shape),
        out_shape=jax.ShapeDtypeStruct(sizes + own.shape, own.dtype),
        in_specs=[VMEM],
        out_specs=VMEM,
        scratch_shapes=[
            pltpu.SemaphoreType.DMA((count,)), pltpu.SemaphoreType.DMA((count,)), pltpu.SemaphoreType.DMA(()),
        ],
        compiler_params=pltpu.CompilerParams(collective_id=0, has_side_effects=True),
        name="gather_days",
    )(own)


def reduce_all(shape, part):
    z, y, x = shape["gz"], shape["gy"], shape["gx"]
    tiles = part.shape[0]
    block = (tiles // (z * y * x),) + part.shape[1:]
    count = 2 * links(shape)
    f32 = jnp.float32
    total = pl.pallas_call(
        functools.partial(reduce_kernel, shape),
        out_shape=jax.ShapeDtypeStruct((z, y, x) + block, f32),
        in_specs=[VMEM],
        out_specs=VMEM,
        scratch_shapes=[
            pltpu.VMEM((z - 1, y, x) + block, f32),
            pltpu.VMEM((y - 1, x) + block, f32),
            pltpu.VMEM((x - 1,) + block, f32),
            pltpu.VMEM((y, x) + block, f32),
            pltpu.VMEM((x,) + block, f32),
            pltpu.SemaphoreType.DMA((count,)),
            pltpu.SemaphoreType.DMA((count,)),
        ],
        compiler_params=pltpu.CompilerParams(collective_id=1, has_side_effects=True),
        name="reduce_all",
    )(part.reshape((z, y, x) + block))
    return total.reshape(part.shape)


def solve_spd(matrix, right):
    lower = jnp.linalg.cholesky(matrix)
    middle = lax.linalg.triangular_solve(lower, right, left_side=True, lower=True)
    return lax.linalg.triangular_solve(lower, middle, left_side=True, lower=True, transpose_a=True)


def dot(left, right, at):
    return lax.dot_general(
        left, right, ((at[:1], at[1:]), ((), ())), precision=lax.Precision.HIGH, preferred_element_type=jnp.float32)


def body(shape, panel, treat_start, loading_init, factor_init, unit_init, day_init):
    unit_rows, total_days = panel.shape
    devices = shape["gx"] * shape["gy"] * shape["gz"]
    all_units = unit_rows * devices
    rank, slice_days = factor_init.shape
    lanes = 128
    across = total_days // lanes
    gram_rows = -(-rank * rank // total_days)
    rows = -(-(rank + gram_rows + 2) // 8) * 8
    while (rows // 8 * across) % devices:
        rows += 8
    ridge_eye = jnp.eye(rank, dtype=jnp.float32) * RIDGE
    observed = lax.broadcasted_iota(jnp.int32, (unit_rows, total_days), 1) < treat_start[:, None]
    loading, unit_eff, day_eff = loading_init, unit_init, day_init
    factors = gather(shape, factor_init).transpose(3, 2, 1, 0, 4).reshape(rank, total_days)
    for _ in range(SWEEPS):
        fitted = dot(loading, factors, (0, 0))
        imputed = jnp.where(observed, panel, unit_eff[:, None] + day_eff[None, :] + fitted)
        without = imputed - fitted
        day_part = jnp.sum(without, 0)
        row_mean = jnp.sum(without, 1) / total_days
        centred = imputed - row_mean[:, None]
        weighted = dot(loading, centred, (1, 0))
        gram = dot(loading, loading, (1, 1)).reshape(-1)
        gram = jnp.pad(gram, (0, gram_rows * total_days - gram.size)).reshape(gram_rows, total_days)
        load_sum = jnp.pad(jnp.sum(loading, 1), (0, total_days - rank))
        part = jnp.concatenate([weighted, day_part[None], load_sum[None], gram], 0)
        part = jnp.pad(part, ((0, rows - part.shape[0]), (0, 0)))
        part = part.reshape(rows // 8, 8, across, lanes).transpose(0, 2, 1, 3).reshape(-1, 8, lanes)
        total = reduce_all(shape, part)
        total = total.reshape(rows // 8, across, 8, lanes).transpose(0, 2, 1, 3).reshape(rows, total_days)
        weighted = total[:rank]
        day_sums = total[rank]
        load_sum = total[rank + 1, :rank]
        gram = total[rank + 2:rank + 2 + gram_rows].reshape(-1)[:rank * rank].reshape(rank, rank)
        grand = jnp.sum(day_sums) / (all_units * total_days)
        day_eff = day_sums / all_units - grand
        unit_eff = row_mean - grand
        shift = (grand - day_eff)[None, :]
        resid = centred + shift
        factors = solve_spd(gram + ridge_eye, weighted + load_sum[:, None] * shift)
        loading = solve_spd(dot(factors, factors, (1, 1)) + ridge_eye, dot(factors, resid, (1, 1)))
    owned = lax.dynamic_slice_in_dim(factors, lax.axis_index(AXES) * slice_days, slice_days, 1)
    return (loading, owned, unit_eff, day_eff)


def solution(mesh):
    return jax.shard_map(
        functools.partial(body, dict(mesh.shape)),
        mesh=mesh,
        in_specs=(P(AXES, None), P(AXES), P(None, AXES), P(None, AXES), P(AXES), P()),
        out_specs=(P(None, AXES), P(None, AXES), P(AXES), P()),
        check_vma=False,
    )
```

profile of v0, /device:TPU:0, one launch (start us, length us, event | category | flops | bytes accessed | tf_op | source)
XLA Modules:
  0.0 184.2 jit_solution(9655058450495885196)
XLA Ops:
  0.7 18.7 %gather_days.1 = f32[2,4,4,64,128]{4,3,2,1,0:T(8,128)} custom-call(f32[64,128]{1,0:T(8,128)} %own_ref.1), custom_call_target="tpu_custom_call" | custom-call | tf_op jit(solution)/shard_map/gather_days/pallas_call | solution.py:98
  19.4 2.0 %copy.16 = f32[64,4,4,2,128]{4,3,2,1,0:T(2,128)S(1)} copy(f32[64,4,4,2,128]{4,0,1,2,3:T(8,128)} %bitcast.131) | data formatting | bytes 2097152 | tf_op jit(solution)/shard_map/transpose | solution.py:162
  21.4 0.8 reshape.82
  22.3 0.0 copy-start
  22.3 5.3 %subtract_reduce_fusion.3 = (f32[256]{0:T(256)S(1)}, f32[4096]{0:T(1024)S(1)}, f32[256,4096]{1,0:T(8,128)S(1)}) fusion(f32[256,4096]{1,0:T(8,128)} %param.15, f32[4096]{0:T(1024)S(1)} %copy-done.5, f32[256]{0:T(256)S(1)} %copy-done.7, s32[256]{0:T(256)S(1)} %copy-done.6, f32[64,256]{1,0:T(8,128)S(1)} %copy-done.4, f32[64,4096]{1,0:T(8,128)S(1)} %reshape.82), kind=kOutput, calls=%fused_computation.22 | convolution fusion | flops 409988864 | bytes 9538560 | tf_op jit(solution)/shard_map/dot_general | solution.py:144
  27.6 0.0 copy-done
  27.6 2.2 %convolution_bitcast_fusion = f32[64,4096]{1,0:T(8,128)S(1)} fusion(f32[64,256]{1,0:T(8,128)S(1)} %copy-done.4, f32[256]{0:T(256)S(1)} %broadcast_multiply_fusion.1, f32[256,4096]{1,0:T(8,128)S(1)} %copy-done, f32[256,4096]{1,0:T(8,128)S(1)} %get-tuple-element.21, f32[4096]{0:T(1024)S(1)} %copy-done.5, f32[256]{0:T(256)S(1)} %copy-done.7, s32[256]{0:T(256)S(1)} %copy-done.6), kind=kOutput, calls=%fused_computation | convolution fusion | flops 407896064 | bytes 9522176 | tf_op jit(solution)/shard_map/dot_general | solution.py:144
  29.8 0.0 copy-done.3
  29.8 0.2 fusion.63
  30.0 0.1 reshape.83
  30.1 0.1 reduce_sum.74
  30.2 1.1 fusion.21
  31.3 33.7 %reduce_all.2 = f32[2,4,4,9,8,128]{5,4,3,2,1,0:T(8,128)} custom-call(f32[2,4,4,9,8,128]{5,4,3,2,1,0:T(8,128)} %bitcast.121), custom_call_target="tpu_custom_call" | custom-call | tf_op jit(solution)/shard_map/reduce_all/pallas_call | solution.py:117
  65.0 1.6 slice_reduce_fusion.1
  66.6 0.1 reshape_reshape.20
  66.7 0.1 copy.17
  66.8 0.1 copy.18
  66.9 5.8 %cholesky.74 = f32[64,64]{1,0:T(8,128)S(1)} custom-call(f32[64,64]{1,0:T(8,128)S(1)} %fusion.55), custom_call_target="Cholesky" | custom-call | tf_op jit(solution)/shard_map/jit(cholesky)/cholesky | solution.py:138
  72.8 0.6 compare_reduce_fusion.3
  73.4 0.7 fusion.34
  74.1 4.9 %custom-call.19 = f32[1,64,64]{1,2,0:T(8,128)S(1)} custom-call(f32[1,64,64]{2,1,0:T(8,128)S(1)} %fusion.34), custom_call_target="InvertDiagBlocksLowerTriangular" | custom-call | tf_op jit(solution)/shard_map/triangular_solve/custom-call.2 | solution.py:140
  79.7 0.9 broadcast_subtract_fusion.1
  80.6 0.7 slice_bitcast_fusion.3
  81.3 2.3 %fusion.26 = f32[64,4096]{1,0:T(8,128)S(1)} fusion(f32[9,8,32,128]{3,1,2,0:T(8,128)} %bitcast.130, f32[4096]{0:T(1024)S(1)} %bitcast.137, f32[64]{0:T(128)S(1)} %slice_bitcast_fusion.3, f32[1,64,64]{1,2,0:T(8,128)S(1)} %custom-call.19), kind=kOutput, calls=%fused_computation.41 | convolution fusion | flops 201850880 | bytes 2130176 | tf_op jit(solution)/shard_map/triangular_solve/dot.1 | solution.py:139
  83.6 1.0 fusion.53
  84.6 0.6 convolution_add_fusion.1
  85.2 0.1 copy.20
  85.3 6.0 %cholesky.85 = f32[64,64]{1,0:T(8,128)S(1)} custom-call(f32[64,64]{1,0:T(8,128)S(1)} %fusion.51), custom_call_target="Cholesky" | custom-call | tf_op jit(solution)/shard_map/jit(cholesky)/cholesky | solution.py:138
  91.3 0.6 compare_reduce_fusion.2
  92.0 0.7 fusion.35
  92.6 4.9 %custom-call.21 = f32[1,64,64]{1,2,0:T(8,128)S(1)} custom-call(f32[1,64,64]{2,1,0:T(8,128)S(1)} %fusion.35), custom_call_target="InvertDiagBlocksLowerTriangular" | custom-call | tf_op jit(solution)/shard_map/triangular_solve/custom-call.4 | solution.py:140
  97.5 0.0 copy-start.1
  97.5 6.3 %fusion.2 = f32[64,256]{1,0:T(8,128)S(1)} fusion(f32[64,4096]{1,0:T(8,128)S(1)} %fusion.53, f32[4096]{0:T(1024)S(1)} %bitcast.138, f32[256]{0:T(256)S(1)} %broadcast_multiply_fusion.1, f32[256,4096]{1,0:T(8,128)} %param.15, f32[256,4096]{1,0:T(8,128)} %copy-done.3, f32[4096]{0:T(1024)S(1)} %copy-done.5, f32[256]{0:T(256)S(1)} %copy-done.7, s32[256]{0:T(256)S(1)} %copy-done.6), kind=kOutput, calls=%fused_computation.4 | convolution fusion | flops 408944640 | bytes 9538560 | tf_op jit(solution)/shard_map/dot_general | solution.py:144
  103.8 0.3 fusion.47
  104.1 0.3 fusion.62
  104.4 3.0 %subtract_reduce_fusion.1 = (f32[256]{0:T(256)S(1)}, f32[4096]{0:T(1024)S(1)}, f32[256,4096]{1,0:T(8,128)S(1)}) fusion(f32[256,4096]{1,0:T(8,128)S(1)} %copy-done.1, f32[4096]{0:T(1024)S(1)} %bitcast.132, f32[256]{0:T(256)S(1)} %broadcast_subtract_fusion.3, s32[256]{0:T(256)S(1)} %copy-done.6, f32[64,256]{1,0:T(8,128)S(1)} %get-tuple-element.23, ...), kind=kOutput, calls=%fused_computation.20 | convolution fusion | flops 409988864 | bytes 9538560 | tf_op jit(solution)/shard_map/dot_general | solution.py:144
  107.5 2.2 %fusion.5 = f32[64,4096]{1,0:T(8,128)S(1)} fusion(f32[64,256]{1,0:T(8,128)S(1)} %get-tuple-element.23, f32[256]{0:T(256)S(1)} %broadcast_multiply_fusion, f32[256,4096]{1,0:T(8,128)S(1)} %copy-done.1, f32[256,4096]{1,0:T(8,128)S(1)} %get-tuple-element.24, f32[4096]{0:T(1024)S(1)} %bitcast.133, f32[256]{0:T(256)S(1)} %broadcast_subtract_fusion.3, ...), kind=kOutput, calls=%fused_computation.9 | convolution fusion | flops 407896064 | bytes 9522176 | tf_op jit(solution)/shard_map/dot_general | solution.py:144
  109.6 0.2 fusion.64
  109.8 0.1 reshape.86
  109.9 1.1 select_maximum_fusion
  111.0 31.5 %reduce_all.3 = f32[2,4,4,9,8,128]{5,4,3,2,1,0:T(8,128)} custom-call(f32[2,4,4,9,8,128]{5,4,3,2,1,0:T(8,128)} %bitcast.122), custom_call_target="tpu_custom_call" | custom-call | tf_op jit(solution)/shard_map/reduce_all/pallas_call | solution.py:117
  142.6 1.6 slice_reduce_fusion
  144.8 0.6 broadcast_subtract_fusion.2
  145.4 0.1 reshape_reshape.23
  145.5 0.1 copy.21
  145.6 0.1 copy.22
  145.7 5.8 %cholesky.96 = f32[64,64]{1,0:T(8,128)S(1)} custom-call(f32[64,64]{1,0:T(8,128)S(1)} %fusion.46), custom_call_target="Cholesky" | custom-call | tf_op jit(solution)/shard_map/jit(cholesky)/cholesky | solution.py:138
  151.6 0.6 compare_reduce_fusion.1
  152.2 0.7 fusion.36
  152.9 4.9 %custom-call.23 = f32[1,64,64]{1,2,0:T(8,128)S(1)} custom-call(f32[1,64,64]{2,1,0:T(8,128)S(1)} %fusion.36), custom_call_target="InvertDiagBlocksLowerTriangular" | custom-call | tf_op jit(solution)/shard_map/triangular_solve/custom-call.2 | solution.py:140
  157.8 1.5 broadcast_subtract_fusion
  159.3 0.7 slice_bitcast_fusion.2
  160.0 2.5 %fusion.23 = f32[64,4096]{1,0:T(8,128)S(1)} fusion(f32[9,8,32,128]{3,1,2,0:T(8,128)} %bitcast.126, f32[4096]{0:T(1024)S(1)} %bitcast.135, f32[64]{0:T(128)S(1)} %slice_bitcast_fusion.2, f32[1,64,64]{1,2,0:T(8,128)S(1)} %custom-call.23), kind=kOutput, calls=%fused_computation.38 | convolution fusion | flops 201850880 | bytes 2130176 | tf_op jit(solution)/shard_map/triangular_solve/dot.1 | solution.py:139
  162.5 1.0 fusion.44
  163.6 0.6 convolution_add_fusion
  164.1 0.1 copy.24
  164.2 5.8 %cholesky.107 = f32[64,64]{1,0:T(8,128)S(1)} custom-call(f32[64,64]{1,0:T(8,128)S(1)} %fusion.42), custom_call_target="Cholesky" | custom-call | tf_op jit(solution)/shard_map/jit(cholesky)/cholesky | solution.py:138
  170.1 0.6 compare_reduce_fusion
  170.8 0.7 fusion.37
  171.4 4.9 %custom-call.25 = f32[1,64,64]{1,2,0:T(8,128)S(1)} custom-call(f32[1,64,64]{2,1,0:T(8,128)S(1)} %fusion.37), custom_call_target="InvertDiagBlocksLowerTriangular" | custom-call | tf_op jit(solution)/shard_map/triangular_solve/custom-call.4 | solution.py:140
  176.3 6.2 %fusion = f32[64,256]{1,0:T(8,128)S(1)} fusion(f32[64,4096]{1,0:T(8,128)S(1)} %fusion.44, f32[4096]{0:T(1024)S(1)} %bitcast.136, f32[256]{0:T(256)S(1)} %broadcast_multiply_fusion, f32[256,4096]{1,0:T(8,128)} %param.15, f32[256,4096]{1,0:T(8,128)} %copy-done.2, f32[4096]{0:T(1024)S(1)} %bitcast.134, f32[256]{0:T(256)S(1)} %broadcast_subtract_fusion.3, ...), kind=kOutput, calls=%fused_computation.1 | convolution fusion | flops 408944640 | bytes 9538560 | tf_op jit(solution)/shard_map/dot_general | solution.py:144
  182.5 0.3 fusion.38
  182.8 0.8 fusion.40
  183.6 0.6 constant_dynamic-slice_fusion
  (27 shorter events, 0.3 us)
Async XLA Ops:
  0.6 21.6 %copy-start.6 = (s32[256]{0:T(256)S(1)}, s32[256]{0:T(256)}, u32[]{:S(2)}) copy-start(s32[256]{0:T(256)} %param.16) | copy-start | bytes 3076
  0.6 21.6 %copy-start.4 = (f32[64,256]{1,0:T(8,128)S(1)}, f32[64,256]{1,0:T(8,128)}, u32[]{:S(2)}) copy-start(f32[64,256]{1,0:T(8,128)} %param.17) | copy-start | bytes 196612
  0.7 21.6 %copy-start.7 = (f32[256]{0:T(256)S(1)}, f32[256]{0:T(256)}, u32[]{:S(2)}) copy-start(f32[256]{0:T(256)} %param.19) | copy-start | bytes 3076
  0.7 21.6 %copy-start.5 = (f32[4096]{0:T(1024)S(1)}, f32[4096]{0:T(1024)}, u32[]{:S(2)}) copy-start(f32[4096]{0:T(1024)} %param.20) | copy-start | bytes 49156
  22.3 5.3 %copy-start = (f32[256,4096]{1,0:T(8,128)S(1)}, f32[256,4096]{1,0:T(8,128)}, u32[]{:S(2)}) copy-start(f32[256,4096]{1,0:T(8,128)} %param.15) | copy-start | bytes 12582916
  27.6 2.3 %copy-start.3 = (f32[256,4096]{1,0:T(8,128)}, f32[256,4096]{1,0:T(8,128)S(1)}, u32[]{:S(2)}) copy-start(f32[256,4096]{1,0:T(8,128)S(1)} %get-tuple-element.21) | copy-start | bytes 12582916
  97.5 6.9 %copy-start.1 = (f32[256,4096]{1,0:T(8,128)S(1)}, f32[256,4096]{1,0:T(8,128)}, u32[]{:S(2)}) copy-start(f32[256,4096]{1,0:T(8,128)} %param.15) | copy-start | bytes 12582916
  107.5 2.2 %copy-start.2 = (f32[256,4096]{1,0:T(8,128)}, f32[256,4096]{1,0:T(8,128)S(1)}, u32[]{:S(2)}) copy-start(f32[256,4096]{1,0:T(8,128)S(1)} %get-tuple-element.24) | copy-start | bytes 12582916
where the time goes:
time: 185 us; the launch traced here: 184 us
  Pallas kernels  83.9 us (45%)
  other arithmetic  57.2 us (31%)
  matrix products  35.2 us (19%)
  local copies, waits for them, and re-layouts  5.67 us (3%)
  between operations  2.34 us (1%)
    pallas_call x2, Pallas kernels, reduce_all(): pl.pallas_call(functools.partial(reduce_kernel, shape), out_shape=jax.Sha...  65.2 us
    dot_general x10, matrix products, dot(): lax.dot_general(left, right, ((at[:1], at[1:]), ((), ())), precision=lax....  26.7 us
    another operation x12, other arithmetic, solve_spd(): lower = jnp.linalg.cholesky(matrix)  26.2 us
    another operation x8, other arithmetic, solve_spd(): lax.linalg.triangular_solve(lower, middle, left_side=True, lower=True, tr...  22.2 us
    pallas_call x1, Pallas kernels, gather(): pl.pallas_call(functools.partial(gather_kernel, shape), out_shape=jax.Sha...  18.7 us
    another operation x4, matrix products, solve_spd(): lax.linalg.triangular_solve(lower, right, left_side=True, lower=True)  5.35 us

commit v1 on v0

--- a/solution.py
+++ b/solution.py
@@ -134,61 +134,174 @@
     return total.reshape(part.shape)
 
 
-def solve_spd(matrix, right):
-    lower = jnp.linalg.cholesky(matrix)
-    middle = lax.linalg.triangular_solve(lower, right, left_side=True, lower=True)
-    return lax.linalg.triangular_solve(lower, middle, left_side=True, lower=True, transpose_a=True)
-
-
-def dot(left, right, at):
-    return lax.dot_general(
-        left, right, ((at[:1], at[1:]), ((), ())), precision=lax.Precision.HIGH, preferred_element_type=jnp.float32)
+def halves(value):
+    high = value.astype(jnp.bfloat16)
+    return high, (value - high.astype(jnp.float32)).astype(jnp.bfloat16)
+
+
+def mul(left, right, at):
+    return lax.dot_general(left, right, ((at[:1], at[1:]), ((), ())), preferred_element_type=jnp.float32)
+
+
+def wide_left(value):
+    high, low = halves(value)
+    return jnp.concatenate([high, high, low], 1)
+
+
+def wide_right(value):
+    high, low = halves(value)
+    return jnp.concatenate([high, low, high], 0)
+
+
+def tall_dot(left, right, at):
+    rows = left.shape[0]
+    left_high, left_low = halves(left)
+    right_high, right_low = halves(right)
+    both = mul(jnp.concatenate([left_high, left_low], 0), right_high, (1, at))
+    return both[:rows] + both[rows:] + mul(left_high, right_low, (1, at))
+
+
+def invert(work):
+    rank = work.shape[0]
+    row_at = lax.broadcasted_iota(jnp.int32, work.shape, 0)
+    for k in range(rank):
+        pivot_row = work[k:k + 1, :] * (1.0 / work[k:k + 1, k:k + 1])
+        work = jnp.where(row_at == k, pivot_row, work - work[:, k:k + 1] * pivot_row)
+    return work[:, rank:]
+
+
+def with_identity(matrix):
+    rank = matrix.shape[0]
+    eye = jnp.where(
+        lax.broadcasted_iota(jnp.int32, (rank, rank), 0) == lax.broadcasted_iota(jnp.int32, (rank, rank), 1), 1.0, 0.0)
+    return jnp.concatenate([matrix + RIDGE * eye, eye], 1)
+
+
+def impute_kernel(width, panel_ref, treat_ref, load_ref, fac_ref, unit_ref, day_ref, part_ref, cent_ref, mean_ref):
+    units, days = panel_ref.shape
+    rank = load_ref.shape[0]
+    lanes = part_ref.shape[2]
+    across = days // lanes
+    each = width // lanes
+    extra = rank // 8 * across
+    per = -(-rank // across)
+    load = load_ref[...]
+    turned = load.T
+    load_wide = wide_left(turned)
+    part_ref[extra:] = jnp.zeros((part_ref.shape[0] - extra,) + part_ref.shape[1:], jnp.float32)
+
+    def first(tile, total):
+        start = pl.multiple_of(tile * width, width)
+        cols = pl.ds(start, width)
+        fitted = mul(load_wide, wide_right(fac_ref[:, cols]), (1, 0))
+        day = lax.broadcasted_iota(jnp.int32, (units, width), 1) + start
+        imputed = jnp.where(day < treat_ref[...], panel_ref[:, cols], unit_ref[...] + day_ref[:, cols] + fitted)
+        cent_ref[:, cols] = imputed
+        without = imputed - fitted
+        sums = jnp.sum(without, 0, keepdims=True)
+        for c in range(each):
+            span = slice(c * lanes, (c + 1) * lanes)
+            part_ref[extra + tile * each + c, 0:1, :] = sums[:, span]
+            total = total + without[:, span]
+        return total
+
+    total = lax.fori_loop(0, days // width, first, jnp.zeros((units, lanes), jnp.float32))
+    mean = jnp.sum(total, 1, keepdims=True) / days
+    mean_ref[...] = mean
+
+    def second(tile, _):
+        cols = pl.ds(pl.multiple_of(tile * width, width), width)
+        centred = cent_ref[:, cols] - mean
+        cent_ref[:, cols] = centred
+        weighted = tall_dot(load, centred, 0)
+        for r in range(rank // 8):
+            for c in range(each):
+                part_ref[r * across + tile * each + c] = weighted[r * 8:r * 8 + 8, c * lanes:(c + 1) * lanes]
+        return 0
+
+    lax.fori_loop(0, days // width, second, 0)
+    gram = tall_dot(load, load, 1)
+    part_ref[extra, 1:2, 0:rank] = jnp.sum(turned, 0, keepdims=True)
+    for c in range(-(-rank // per)):
+        part_ref[extra + c, 2:2 + per, 0:rank] = gram[c * per:(c + 1) * per]
+
+
+def solve_kernel(width, devices, total_ref, cent_ref, mean_ref, load_ref, fac_ref, unit_ref, day_ref, gram, shift):
+    units, days = cent_ref.shape
+    rank = load_ref.shape[0]
+    lanes = total_ref.shape[2]
+    across = days // lanes
+    each = width // lanes
+    extra = rank // 8 * across
+    per = -(-rank // across)
+    for c in range(across):
+        shift[0:1, c * lanes:(c + 1) * lanes] = total_ref[extra + c, 0:1, :]
+    for c in range(-(-rank // per)):
+        gram[c * per:(c + 1) * per, :] = total_ref[extra + c, 2:2 + per, :]
+    sums = shift[...]
+    grand = jnp.sum(sums, 1, keepdims=True) / (units * devices * days)
+    day_eff = sums / (units * devices) - grand
+    day_ref[...] = day_eff
+    shift[...] = grand - day_eff
+    unit_ref[...] = mean_ref[...] - grand
+    inverse = wide_left(invert(with_identity(gram[:, 0:rank])))
+    same = lax.broadcasted_iota(jnp.int32, (rank, rank), 0) == lax.broadcasted_iota(jnp.int32, (rank, rank), 1)
+    load_sum = jnp.sum(jnp.where(same, total_ref[extra, 1:2, 0:rank], 0.0), 1, keepdims=True)
+
+    def step(tile, carry):
+        square, projected = carry
+        cols = pl.ds(pl.multiple_of(tile * width, width), width)
+        weighted = jnp.concatenate([
+            jnp.concatenate([total_ref[r * across + tile * each + c] for c in range(each)], 1)
+            for r in range(rank // 8)], 0)
+        moved = shift[:, cols]
+        factors = mul(inverse, wide_right(weighted + load_sum * moved), (1, 0))
+        fac_ref[:, cols] = factors
+        square = square + tall_dot(factors, factors, 1)
+        projected = projected + tall_dot(factors, cent_ref[:, cols] + moved, 1)
+        return square, projected
+
+    square, projected = lax.fori_loop(
+        0, days // width, step, (jnp.zeros((rank, rank), jnp.float32), jnp.zeros((rank, units), jnp.float32)))
+    load_ref[...] = mul(wide_left(invert(with_identity(square))), wide_right(projected), (1, 0))
 
 
 def body(shape, panel, treat_start, loading_init, factor_init, unit_init, day_init):
-    unit_rows, total_days = panel.shape
+    units, days = panel.shape
     devices = shape["gx"] * shape["gy"] * shape["gz"]
-    all_units = unit_rows * devices
     rank, slice_days = factor_init.shape
     lanes = 128
-    across = total_days // lanes
-    gram_rows = -(-rank * rank // total_days)
-    rows = -(-(rank + gram_rows + 2) // 8) * 8
-    while (rows // 8 * across) % devices:
-        rows += 8
-    ridge_eye = jnp.eye(rank, dtype=jnp.float32) * RIDGE
-    observed = lax.broadcasted_iota(jnp.int32, (unit_rows, total_days), 1) < treat_start[:, None]
-    loading, unit_eff, day_eff = loading_init, unit_init, day_init
-    factors = gather(shape, factor_init).transpose(3, 2, 1, 0, 4).reshape(rank, total_days)
+    tiles = (rank // 8 + 1) * (days // lanes)
+    tiles = -(-tiles // devices) * devices
+    width = min(512, days)
+    f32 = jnp.float32
+
+    def array(*sizes):
+        return jax.ShapeDtypeStruct(sizes, f32)
+
+    impute = pl.pallas_call(
+        functools.partial(impute_kernel, width),
+        out_shape=(array(tiles, 8, lanes), array(units, days), array(units, 1)),
+        in_specs=[VMEM] * 6,
+        out_specs=(VMEM,) * 3,
+        name="impute",
+    )
+    solve = pl.pallas_call(
+        functools.partial(solve_kernel, width, devices),
+        out_shape=(array(rank, units), array(rank, days), array(units, 1), array(1, days)),
+        in_specs=[VMEM] * 3,
+        out_specs=(VMEM,) * 4,
+        scratch_shapes=[pltpu.VMEM((rank, lanes), f32), pltpu.VMEM((1, days), f32)],
+        name="solve",
+    )
+    treat = treat_start[:, None]
+    loading, unit_eff, day_eff = loading_init, unit_init[:, None], day_init[None, :]
+    factors = gather(shape, factor_init).transpose(3, 2, 1, 0, 4).reshape(rank, days)
     for _ in range(SWEEPS):
-        fitted = dot(loading, factors, (0, 0))
-        imputed = jnp.where(observed, panel, unit_eff[:, None] + day_eff[None, :] + fitted)
-        without = imputed - fitted
-        day_part = jnp.sum(without, 0)
-        row_mean = jnp.sum(without, 1) / total_days
-        centred = imputed - row_mean[:, None]
-        weighted = dot(loading, centred, (1, 0))
-        gram = dot(loading, loading, (1, 1)).reshape(-1)
-        gram = jnp.pad(gram, (0, gram_rows * total_days - gram.size)).reshape(gram_rows, total_days)
-        load_sum = jnp.pad(jnp.sum(loading, 1), (0, total_days - rank))
-        part = jnp.concatenate([weighted, day_part[None], load_sum[None], gram], 0)
-        part = jnp.pad(part, ((0, rows - part.shape[0]), (0, 0)))
-        part = part.reshape(rows // 8, 8, across, lanes).transpose(0, 2, 1, 3).reshape(-1, 8, lanes)
-        total = reduce_all(shape, part)
-        total = total.reshape(rows // 8, across, 8, lanes).transpose(0, 2, 1, 3).reshape(rows, total_days)
-        weighted = total[:rank]
-        day_sums = total[rank]
-        load_sum = total[rank + 1, :rank]
-        gram = total[rank + 2:rank + 2 + gram_rows].reshape(-1)[:rank * rank].reshape(rank, rank)
-        grand = jnp.sum(day_sums) / (all_units * total_days)
-        day_eff = day_sums / all_units - grand
-        unit_eff = row_mean - grand
-        shift = (grand - day_eff)[None, :]
-        resid = centred + shift
-        factors = solve_spd(gram + ridge_eye, weighted + load_sum[:, None] * shift)
-        loading = solve_spd(dot(factors, factors, (1, 1)) + ridge_eye, dot(factors, resid, (1, 1)))
+        part, centred, mean = impute(panel, treat, loading, factors, unit_eff, day_eff)
+        loading, factors, unit_eff, day_eff = solve(reduce_all(shape, part), centred, mean)
     owned = lax.dynamic_slice_in_dim(factors, lax.axis_index(AXES) * slice_days, slice_days, 1)
-    return (loading, owned, unit_eff, day_eff)
+    return (loading, owned, unit_eff[:, 0], day_eff[0])
 
 
 def solution(mesh):

time: 185 us -> 150 us (0.81)
  Pallas kernels: 83.9 us -> 140 us
  other arithmetic: 57.2 us -> 1.58 us
  matrix products: 35.2 us -> 0 us
    pallas_call x0 -> x4, Pallas kernels: none -> 56.2 us  [the longest x2 37.2 us: body(): solve(reduce_all(shape, part), centred, mean)]
    another operation x20 -> x0, other arithmetic: 48.4 us -> none  [the longest x12 26.2 us: solve_spd(): lower = jnp.linalg.cholesky(matrix)]
    dot_general x10 -> x0, matrix products: 26.7 us -> none  [dot(): lax.dot_general(left, right, ((at[:1], at[1:]), ((), ())), precision=lax....]
    another operation x8 -> x0, matrix products: 8.49 us -> none  [the longest x4 5.35 us: solve_spd(): lax.linalg.triangular_solve(lower, right, left_side=True, lower=True)]
    slice x2 -> x0, other arithmetic: 3.26 us -> none  [body(): total[rank + 2:rank + 2 + gram_rows].reshape(-1)[:rank * rank]]
    sub x4 -> x0, other arithmetic: 3.04 us -> none  [the longest x2 2.47 us: body(): shift = (grand - day_eff)[None, :]]
    broadcast_in_dim x0 -> x2, local copies, waits for them, and re-layouts: none -> 2.27 us  [the longest x1 1.47 us: body(): treat = treat_start[:, None]]
    concatenate x2 -> x0, other arithmetic: 2.23 us -> none  [body(): part = jnp.concatenate([weighted, day_part[None], load_sum[None], gram], 0)]
where the time goes in v1:
time: 150 us
  Pallas kernels  140 us (93%)
  local copies, waits for them, and re-layouts  7.5 us (5%)
  other arithmetic  1.58 us (1%)
    pallas_call x2, Pallas kernels, reduce_all(): pl.pallas_call(functools.partial(reduce_kernel, shape), out_shape=jax.Sha...  65.1 us
    pallas_call x2, Pallas kernels, body(): solve(reduce_all(shape, part), centred, mean)  37.2 us
    pallas_call x2, Pallas kernels, body(): impute(panel, treat, loading, factors, unit_eff, day_eff)  19.1 us
    pallas_call x1, Pallas kernels, gather(): pl.pallas_call(functools.partial(gather_kernel, shape), out_shape=jax.Sha...  18.6 us

profile of v1, /device:TPU:0, one launch (start us, length us, event | category | flops | bytes accessed | tf_op | source)
XLA Modules:
  0.0 149.7 jit_solution(14728691954506657777)
XLA Ops:
  0.6 1.5 copy.14.treat_ref
  2.1 18.6 %gather_days.1 = f32[2,4,4,64,128]{4,3,2,1,0:T(8,128)} custom-call(f32[64,128]{1,0:T(8,128)} %own_ref.1), custom_call_target="tpu_custom_call" | custom-call | tf_op jit(solution)/shard_map/gather_days/pallas_call | solution.py:98
  20.7 2.0 %copy.11 = f32[64,4,4,2,128]{4,3,2,1,0:T(2,128)S(1)} copy(f32[64,4,4,2,128]{4,0,1,2,3:T(8,128)} %bitcast.11) | data formatting | bytes 2097152 | tf_op jit(solution)/shard_map/transpose | solution.py:299
  22.8 0.0 copy-start
  22.8 1.8 %reshape.23.fac_ref = f32[64,4096]{1,0:T(8,128)} reshape(f32[64,4,4,2,128]{4,3,2,1,0:T(2,128)S(1)} %copy.11) | data formatting | bytes 2097152 | tf_op jit(solution)/shard_map/reshape | solution.py:299
  24.6 0.0 copy-done
  24.6 0.8 copy.13.unit_ref
  25.4 9.5 %impute.2 = (f32[288,8,128]{2,1,0:T(8,128)}, f32[256,4096]{1,0:T(8,128)}, f32[256,1]{1,0:T(8,128)}) custom-call(f32[256,4096]{1,0:T(8,128)} %panel_ref.3, s32[256,1]{1,0:T(8,128)} %copy.14.treat_ref, f32[64,256]{1,0:T(8,128)} %load_ref.1, f32[64,4096]{1,0:T(8,128)} %reshape.23.fac_ref, f32[256,1]{1,0:T(8,128)} %copy.13.unit_ref, f32[1,4096]{1,0:T(1,128)} %bitcast.14), custom_call_target="tpu_custom_call" | custom-call | tf_op jit(solution)/shard_map/impute/pallas_call | solution.py:301
  34.9 33.6 %reduce_all.2 = f32[2,4,4,9,8,128]{5,4,3,2,1,0:T(8,128)} custom-call(f32[2,4,4,9,8,128]{5,4,3,2,1,0:T(8,128)} %bitcast.13), custom_call_target="tpu_custom_call" | custom-call | tf_op jit(solution)/shard_map/reduce_all/pallas_call | solution.py:117
  68.6 18.6 %solve.2 = (f32[64,256]{1,0:T(8,128)}, f32[64,4096]{1,0:T(8,128)}, f32[256,1]{1,0:T(8,128)}, f32[1,4096]{1,0:T(1,128)}) custom-call(f32[288,8,128]{2,1,0:T(8,128)} %bitcast.9, f32[256,4096]{1,0:T(8,128)} %get-tuple-element.19.cent_ref, f32[256,1]{1,0:T(8,128)} %get-tuple-element.20.mean_ref), custom_call_target="tpu_custom_call" | custom-call | tf_op jit(solution)/shard_map/solve/pallas_call | solution.py:302
  87.2 9.5 %impute.3 = (f32[288,8,128]{2,1,0:T(8,128)}, f32[256,4096]{1,0:T(8,128)}, f32[256,1]{1,0:T(8,128)}) custom-call(f32[256,4096]{1,0:T(8,128)} %panel_ref.3, s32[256,1]{1,0:T(8,128)} %copy.14.treat_ref, f32[64,256]{1,0:T(8,128)} %get-tuple-element.21.load_ref, f32[64,4096]{1,0:T(8,128)} %get-tuple-element.22.fac_ref, f32[256,1]{1,0:T(8,128)} %get-tuple-element.23.unit_ref, ...), custom_call_target="tpu_custom_call" | custom-call | tf_op jit(solution)/shard_map/impute/pallas_call | solution.py:301
  96.7 31.5 %reduce_all.3 = f32[2,4,4,9,8,128]{5,4,3,2,1,0:T(8,128)} custom-call(f32[2,4,4,9,8,128]{5,4,3,2,1,0:T(8,128)} %bitcast.12), custom_call_target="tpu_custom_call" | custom-call | tf_op jit(solution)/shard_map/reduce_all/pallas_call | solution.py:117
  128.2 18.6 %solve.3 = (f32[64,256]{1,0:T(8,128)}, f32[64,4096]{1,0:T(8,128)}, f32[256,1]{1,0:T(8,128)}, f32[1,4096]{1,0:T(1,128)}) custom-call(f32[288,8,128]{2,1,0:T(8,128)} %bitcast.10, f32[256,4096]{1,0:T(8,128)} %get-tuple-element.26.cent_ref, f32[256,1]{1,0:T(8,128)} %get-tuple-element.27.mean_ref), custom_call_target="tpu_custom_call" | custom-call | tf_op jit(solution)/shard_map/solve/pallas_call | solution.py:302
  146.8 1.4 constant_dynamic-slice_fusion
  148.1 1.6 %reduce = f32[256]{0:T(256)} reduce(f32[256,1]{1,0:T(8,128)} %get-tuple-element.30, f32[]{:T(128)} %constant.21), dimensions={1}, to_apply=%get-tuple-element.30.reduce_sub_computation | reduce | bytes 2052 | tf_op jit(solution)/shard_map/solve/pallas_call | solution.py:302
Async XLA Ops:
  22.8 1.8 %copy-start = (f32[256]{0:T(256)S(1)}, f32[256]{0:T(256)}, u32[]{:S(2)}) copy-start(f32[256]{0:T(256)} %param.10) | copy-start | bytes 3076

commit v2 on v1

--- a/solution.py
+++ b/solution.py
@@ -9,6 +9,8 @@
 
 SWEEPS = 2
 RIDGE = 1.0
+GATHER_PIECES = 2
+REDUCE_PIECES = 3
 AXES = ("gx", "gy", "gz")
 MESH = pl.DeviceIdType.MESH
 VMEM = pl.BlockSpec(memory_space=pltpu.VMEM)
@@ -36,56 +38,91 @@
     pl.semaphore_wait(barrier, count)
 
 
-def spread(out_ref, here, found, send, recv, base):
-    index = base
-    for depth, axis in ((3, "gx"), (2, "gy"), (1, "gz")):
-        at = (here["gz"], here["gy"], here["gx"])[:depth]
-        mine = out_ref.at[at]
-        copies = []
-        for _, _, device in found[axis]:
-            copies.append(pltpu.make_async_remote_copy(
-                mine, mine, send.at[index], recv.at[index], device_id=device, device_id_type=MESH))
-            index += 1
-        for copy in copies:
-            copy.start()
-        for copy in copies:
-            copy.wait()
-
-
-def gather_kernel(shape, own_ref, out_ref, send, recv, local):
+def send_all(found, source, target, send, recv, base):
+    copies = []
+    for slot, (step, there, device) in enumerate(found):
+        copies.append(pltpu.make_async_remote_copy(
+            source(step, there), target(step), send.at[base + slot], recv.at[base + slot],
+            device_id=device, device_id_type=MESH))
+    for copy in copies:
+        copy.start()
+    return copies
+
+
+def finish(copies):
+    for copy in copies:
+        copy.wait()
+
+
+def spread(block, place, found, send, recv, base):
+    mine = block.at[place]
+    return send_all(found, lambda step, there: mine, lambda step: mine, send, recv, base)
+
+
+def gather_kernel(shape, own_ref, out_ref, blocks, send, recv, local):
     here, found = peers(shape)
-    copy = pltpu.make_async_copy(own_ref, out_ref.at[here["gz"], here["gy"], here["gx"]], local)
-    copy.start()
+    z, y, x = here["gz"], here["gy"], here["gx"]
+    pieces, rows = blocks.shape[0], blocks.shape[4]
+    width = own_ref.shape[1]
+    starts = []
+    for p in range(pieces):
+        starts.append(pltpu.make_async_copy(own_ref.at[p * rows:(p + 1) * rows], blocks.at[p, z, y, x], local.at[p]))
+        starts[p].start()
     meet(found)
-    copy.wait()
-    spread(out_ref, here, found, send, recv, 0)
+    moving = [[copy] for copy in starts]
+    index = 0
+    for axis, place in (("gx", (z, y, x)), ("gy", (z, y)), ("gz", (z,))):
+        for p in range(pieces):
+            finish(moving[p])
+            moving[p] = spread(blocks.at[p], place, found[axis], send, recv, index)
+            index += len(found[axis])
+    for p in range(pieces):
+        finish(moving[p])
+        flat = 0
+        for x in range(shape["gx"]):
+            for y in range(shape["gy"]):
+                for z in range(shape["gz"]):
+                    out_ref[p * rows:(p + 1) * rows, flat * width:(flat + 1) * width] = blocks[p, z, y, x]
+                    flat += 1
 
 
 def reduce_kernel(shape, part_ref, out_ref, hold_z, hold_y, hold_x, sum_z, sum_y, send, recv):
     here, found = peers(shape)
+    z, y, x = here["gz"], here["gy"], here["gx"]
+    pieces = part_ref.shape[0]
     meet(found)
-    source = part_ref
     index = 0
-    for axis, hold, total in (("gz", hold_z, sum_z), ("gy", hold_y, sum_y), ("gx", hold_x, None)):
-        copies = []
-        for step, there, device in found[axis]:
-            copies.append(pltpu.make_async_remote_copy(
-                source.at[there], hold.at[step - 1], send.at[index], recv.at[index],
-                device_id=device, device_id_type=MESH))
-            index += 1
-        for copy in copies:
-            copy.start()
-        for copy in copies:
-            copy.wait()
-        value = source[here[axis]]
-        for slot in range(len(copies)):
-            value = value + hold[slot]
-        if total is None:
-            out_ref[here["gz"], here["gy"], here["gx"]] = value
-        else:
-            total[...] = value
-            source = total
-    spread(out_ref, here, found, send, recv, index)
+    moving = [[] for _ in range(pieces)]
+    for axis, source, hold in (("gz", part_ref, hold_z), ("gy", sum_z, hold_y), ("gx", sum_y, hold_x)):
+        for p in range(pieces):
+            if axis == "gy":
+                finish(moving[p])
+                value = part_ref[p, z]
+                for slot in range(shape["gz"] - 1):
+                    value = value + hold_z[p, slot]
+                sum_z[p] = value
+            if axis == "gx":
+                finish(moving[p])
+                value = sum_z[p, y]
+                for slot in range(shape["gy"] - 1):
+                    value = value + hold_y[p, slot]
+                sum_y[p] = value
+            moving[p] = send_all(
+                found[axis], lambda step, there: source.at[p, there], lambda step: hold.at[p, step - 1],
+                send, recv, index)
+            index += len(found[axis])
+    for axis, place in (("gx", (z, y, x)), ("gy", (z, y)), ("gz", (z,))):
+        for p in range(pieces):
+            finish(moving[p])
+            if axis == "gx":
+                value = sum_y[p, x]
+                for slot in range(shape["gx"] - 1):
+                    value = value + hold_x[p, slot]
+                out_ref[p, z, y, x] = value
+            moving[p] = spread(out_ref.at[p], place, found[axis], send, recv, index)
+            index += len(found[axis])
+    for p in range(pieces):
+        finish(moving[p])
 
 
 def links(shape):
@@ -93,15 +130,18 @@
 
 
 def gather(shape, own):
-    sizes = (shape["gz"], shape["gy"], shape["gx"])
-    count = links(shape)
+    pieces = GATHER_PIECES
+    rows, width = own.shape
+    devices = shape["gx"] * shape["gy"] * shape["gz"]
+    count = pieces * links(shape)
     return pl.pallas_call(
         functools.partial(gather_kernel, shape),
-        out_shape=jax.ShapeDtypeStruct(sizes + own.shape, own.dtype),
+        out_shape=jax.ShapeDtypeStruct((rows, devices * width), own.dtype),
         in_specs=[VMEM],
         out_specs=VMEM,
         scratch_shapes=[
-            pltpu.SemaphoreType.DMA((count,)), pltpu.SemaphoreType.DMA((count,)), pltpu.SemaphoreType.DMA(()),
+            pltpu.VMEM((pieces, shape["gz"], shape["gy"], shape["gx"], rows // pieces, width), own.dtype),
+            pltpu.SemaphoreType.DMA((count,)), pltpu.SemaphoreType.DMA((count,)), pltpu.SemaphoreType.DMA((pieces,)),
         ],
         compiler_params=pltpu.CompilerParams(collective_id=0, has_side_effects=True),
         name="gather_days",
@@ -110,27 +150,28 @@
 
 def reduce_all(shape, part):
     z, y, x = shape["gz"], shape["gy"], shape["gx"]
+    pieces = REDUCE_PIECES
     tiles = part.shape[0]
-    block = (tiles // (z * y * x),) + part.shape[1:]
-    count = 2 * links(shape)
+    block = (tiles // (pieces * z * y * x),) + part.shape[1:]
+    count = 2 * pieces * links(shape)
     f32 = jnp.float32
     total = pl.pallas_call(
         functools.partial(reduce_kernel, shape),
-        out_shape=jax.ShapeDtypeStruct((z, y, x) + block, f32),
+        out_shape=jax.ShapeDtypeStruct((pieces, z, y, x) + block, f32),
         in_specs=[VMEM],
         out_specs=VMEM,
         scratch_shapes=[
-            pltpu.VMEM((z - 1, y, x) + block, f32),
-            pltpu.VMEM((y - 1, x) + block, f32),
-            pltpu.VMEM((x - 1,) + block, f32),
-            pltpu.VMEM((y, x) + block, f32),
-            pltpu.VMEM((x,) + block, f32),
+            pltpu.VMEM((pieces, z - 1, y, x) + block, f32),
+            pltpu.VMEM((pieces, y - 1, x) + block, f32),
+            pltpu.VMEM((pieces, x - 1) + block, f32),
+            pltpu.VMEM((pieces, y, x) + block, f32),
+            pltpu.VMEM((pieces, x) + block, f32),
             pltpu.SemaphoreType.DMA((count,)),
             pltpu.SemaphoreType.DMA((count,)),
         ],
         compiler_params=pltpu.CompilerParams(collective_id=1, has_side_effects=True),
         name="reduce_all",
-    )(part.reshape((z, y, x) + block))
+    )(part.reshape((pieces, z, y, x) + block))
     return total.reshape(part.shape)
 
 
@@ -272,7 +313,7 @@
     rank, slice_days = factor_init.shape
     lanes = 128
     tiles = (rank // 8 + 1) * (days // lanes)
-    tiles = -(-tiles // devices) * devices
+    tiles = -(-tiles // (REDUCE_PIECES * devices)) * REDUCE_PIECES * devices
     width = min(512, days)
     f32 = jnp.float32
 
@@ -296,7 +337,7 @@
     )
     treat = treat_start[:, None]
     loading, unit_eff, day_eff = loading_init, unit_init[:, None], day_init[None, :]
-    factors = gather(shape, factor_init).transpose(3, 2, 1, 0, 4).reshape(rank, days)
+    factors = gather(shape, factor_init)
     for _ in range(SWEEPS):
         part, centred, mean = impute(panel, treat, loading, factors, unit_eff, day_eff)
         loading, factors, unit_eff, day_eff = solve(reduce_all(shape, part), centred, mean)

time: 150 us -> 137 us (0.913)
  Pallas kernels: 140 us -> 131 us
  local copies, waits for them, and re-layouts: 7.5 us -> 3.65 us
    pallas_call x2, Pallas kernels: 65.1 us -> 56.3 us  [reduce_all(): pl.pallas_call(functools.partial(reduce_kernel, shape), out_shape=jax.Sha...]
    transpose x1 -> x0, local copies, waits for them, and re-layouts: 2.04 us -> none  [body(): gather(shape, factor_init).transpose(3, 2, 1, 0, 4).reshape(rank, days)]
    reshape x1 -> x0, local copies, waits for them, and re-layouts: 1.82 us -> none  [body(): gather(shape, factor_init).transpose(3, 2, 1, 0, 4).reshape(rank, days)]
where the time goes in v2:
time: 137 us
  Pallas kernels  131 us (96%)
  local copies, waits for them, and re-layouts  3.65 us (3%)
  other arithmetic  1.58 us (1%)
    pallas_call x2, Pallas kernels, reduce_all(): pl.pallas_call(functools.partial(reduce_kernel, shape), out_shape=jax.Sha...  56.3 us
    pallas_call x2, Pallas kernels, body(): solve(reduce_all(shape, part), centred, mean)  37.2 us
    pallas_call x2, Pallas kernels, body(): impute(panel, treat, loading, factors, unit_eff, day_eff)  19.1 us
    pallas_call x1, Pallas kernels, gather(): pl.pallas_call(functools.partial(gather_kernel, shape), out_shape=jax.Sha...  18.2 us

profile of v2, /device:TPU:0, one launch (start us, length us, event | category | flops | bytes accessed | tf_op | source)
XLA Modules:
  0.0 136.6 jit_solution(6254223505193599300)
XLA Ops:
  0.6 0.0 copy-start
  0.6 1.5 %copy.12.treat_ref = s32[256,1]{1,0:T(8,128)} copy(s32[256,1]{0,1:T(1,128)} %bitcast.13) | data formatting | bytes 2048 | tf_op jit(solution)/shard_map/broadcast_in_dim | solution.py:338
  2.1 18.2 %gather_days.1.fac_ref = f32[64,4096]{1,0:T(8,128)} custom-call(f32[64,128]{1,0:T(8,128)} %own_ref.1), custom_call_target="tpu_custom_call" | custom-call | tf_op jit(solution)/shard_map/gather_days/pallas_call | solution.py:137
  20.3 0.0 copy-done
  20.3 0.8 copy.11.unit_ref
  21.1 9.5 %impute.2 = (f32[288,8,128]{2,1,0:T(8,128)}, f32[256,4096]{1,0:T(8,128)}, f32[256,1]{1,0:T(8,128)}) custom-call(f32[256,4096]{1,0:T(8,128)} %panel_ref.3, s32[256,1]{1,0:T(8,128)} %copy.12.treat_ref, f32[64,256]{1,0:T(8,128)} %load_ref.1, f32[64,4096]{1,0:T(8,128)} %gather_days.1.fac_ref, f32[256,1]{1,0:T(8,128)} %copy.11.unit_ref, f32[1,4096]{1,0:T(1,128)} %bitcast.12), custom_call_target="tpu_custom_call" | custom-call | tf_op jit(solution)/shard_map/impute/pallas_call | solution.py:342
  30.7 28.7 %reduce_all.2 = f32[3,2,4,4,3,8,128]{6,5,4,3,2,1,0:T(8,128)} custom-call(f32[3,2,4,4,3,8,128]{6,5,4,3,2,1,0:T(8,128)} %bitcast.11), custom_call_target="tpu_custom_call" | custom-call | tf_op jit(solution)/shard_map/reduce_all/pallas_call | solution.py:158
  59.4 18.6 %solve.2 = (f32[64,256]{1,0:T(8,128)}, f32[64,4096]{1,0:T(8,128)}, f32[256,1]{1,0:T(8,128)}, f32[1,4096]{1,0:T(1,128)}) custom-call(f32[288,8,128]{2,1,0:T(8,128)} %bitcast.8, f32[256,4096]{1,0:T(8,128)} %get-tuple-element.19.cent_ref, f32[256,1]{1,0:T(8,128)} %get-tuple-element.20.mean_ref), custom_call_target="tpu_custom_call" | custom-call | tf_op jit(solution)/shard_map/solve/pallas_call | solution.py:343
  78.0 9.5 %impute.3 = (f32[288,8,128]{2,1,0:T(8,128)}, f32[256,4096]{1,0:T(8,128)}, f32[256,1]{1,0:T(8,128)}) custom-call(f32[256,4096]{1,0:T(8,128)} %panel_ref.3, s32[256,1]{1,0:T(8,128)} %copy.12.treat_ref, f32[64,256]{1,0:T(8,128)} %get-tuple-element.21.load_ref, f32[64,4096]{1,0:T(8,128)} %get-tuple-element.22.fac_ref, f32[256,1]{1,0:T(8,128)} %get-tuple-element.23.unit_ref, ...), custom_call_target="tpu_custom_call" | custom-call | tf_op jit(solution)/shard_map/impute/pallas_call | solution.py:342
  87.5 27.5 %reduce_all.3 = f32[3,2,4,4,3,8,128]{6,5,4,3,2,1,0:T(8,128)} custom-call(f32[3,2,4,4,3,8,128]{6,5,4,3,2,1,0:T(8,128)} %bitcast.10), custom_call_target="tpu_custom_call" | custom-call | tf_op jit(solution)/shard_map/reduce_all/pallas_call | solution.py:158
  115.0 18.6 %solve.3 = (f32[64,256]{1,0:T(8,128)}, f32[64,4096]{1,0:T(8,128)}, f32[256,1]{1,0:T(8,128)}, f32[1,4096]{1,0:T(1,128)}) custom-call(f32[288,8,128]{2,1,0:T(8,128)} %bitcast.9, f32[256,4096]{1,0:T(8,128)} %get-tuple-element.26.cent_ref, f32[256,1]{1,0:T(8,128)} %get-tuple-element.27.mean_ref), custom_call_target="tpu_custom_call" | custom-call | tf_op jit(solution)/shard_map/solve/pallas_call | solution.py:343
  133.6 1.4 %constant_dynamic-slice_fusion = f32[64,128]{1,0:T(8,128)} fusion(f32[64,4096]{1,0:T(8,128)} %get-tuple-element.29, s32[]{:T(128)S(6)} %select_n.3), kind=kLoop, calls=%fused_computation | loop fusion | bytes 65540 | tf_op jit(solution)/shard_map/dynamic_slice | solution.py:344
  135.0 1.6 %reduce = f32[256]{0:T(256)} reduce(f32[256,1]{1,0:T(8,128)} %get-tuple-element.30, f32[]{:T(128)} %constant.21), dimensions={1}, to_apply=%get-tuple-element.30.reduce_sub_computation | reduce | bytes 2052 | tf_op jit(solution)/shard_map/solve/pallas_call | solution.py:343
Async XLA Ops:
  0.6 19.7 %copy-start = (f32[256]{0:T(256)S(1)}, f32[256]{0:T(256)}, u32[]{:S(2)}) copy-start(f32[256]{0:T(256)} %param.10) | copy-start | bytes 3076
